TPU v7x, 256 devices: a whole 4x4x8 slice. The times are simulated.
256 devices in a mesh: row: 32 (over x, z_hi, core), col: 8 (over z_lo, y).
Axes of the slice: x: 4, y: 4, z: 8 (z_hi: 4, z_lo: 2; z = z_hi * 2 + z_lo), core: 2. Of those that a mesh axis runs over, the one named last changes fastest.
Arguments:
- amplitudes: float32 [32, 8, 1024, 1024], P('row', 'col'), may hold values from -6 to 6
- panels_left: bfloat16 [32, 2, 1024, 1024], P('row', None, 'col'), may hold values from -6 to 6
- panels_right: bfloat16 [8, 2, 1024, 1024], P('col', None, 'row'), may hold values from -6 to 6
- weights_right: bfloat16 [2, 8, 1024, 1024], P(None, 'col', 'row'), may hold values from -0.125 to 0.125
- weights_left: bfloat16 [2, 32, 1024, 1024], P(None, 'row', 'col'), may hold values from -0.125 to 0.125
- energy_left: float32 [32], P('row'), may hold values from -2 to -0.5
- energy_right: float32 [8], P('col'), may hold values from -2 to -0.5
- energy_virtual: float32 [1024], replicated, may hold values from 0.5 to 3
Outputs:
- updated: float32 [32, 8, 1024, 1024], P('row', 'col')
All inputs are finite; a program needn't handle non-finite values.
Results may differ from a plain program's by a relative error of at most 0.0018.
Values may be sent and summed in bfloat16 or wider, within the bound.
A program may use at most 128 MiB of HBM per device.

v0:
```python
import jax
import jax.numpy as jnp
from jax import lax
from jax.sharding import PartitionSpec as P


def combine_blocks(blocks):
    as_float = blocks.astype(jnp.float32)
    return (2.0 * as_float - jnp.swapaxes(as_float, -1, -2)).astype(jnp.bfloat16)


def body(
    amplitudes,
    panels_left,
    panels_right,
    weights_right,
    weights_left,
    energy_left,
    energy_right,
    energy_virtual,
):
    left_slab = panels_left[0]
    right_slab = panels_right[0]
    right_weight_slab = weights_right[:, 0]
    left_weight_slab = weights_left[:, 0]
    left_whole = lax.all_gather(left_slab, "col", axis=1, tiled=True)
    left_mixed = combine_blocks(left_whole)
    mixed_cols = left_mixed
    direct = jnp.einsum(
        "kac,kcb->ab",
        mixed_cols,
        lax.all_gather(right_weight_slab, "row", axis=1, tiled=True),
        preferred_element_type=jnp.float32,
    )
    right_whole = lax.all_gather(right_slab, "row", axis=1, tiled=True)
    right_mixed = combine_blocks(right_whole)
    mixed_cols = right_mixed
    mirror = jnp.einsum(
        "kac,kcb->ab",
        mixed_cols,
        lax.all_gather(left_weight_slab, "col", axis=1, tiled=True),
        preferred_element_type=jnp.float32,
    )
    residual = direct + jnp.transpose(mirror)
    virt_pair = energy_virtual[:, None] + energy_virtual[None, :]
    denominator = energy_left[0] + energy_right[0] - virt_pair
    return (amplitudes[0, 0] + residual / denominator)[None, None]


def solution(mesh):
    placed = (
        P("row", "col", None, None),
        P("row", None, "col", None),
        P("col", None, "row", None),
        P(None, "col", "row", None),
        P(None, "row", "col", None),
        P("row"),
        P("col"),
        P(),
    )
    return jax.shard_map(
        body, mesh=mesh, in_specs=placed, out_specs=P("row", "col", None, None), check_vma=False
    )
```

profile of v0, /device:TPU:1, one launch (start us, length us, event | category | flops | bytes accessed | tf_op | source)
XLA Modules:
  0.0 267.6 jit_solution(162221997629663721)
XLA Ops:
  6.5 0.0 all-gather.9.cloned.1.call-start
  6.5 0.7 all-gather.9.cloned.1.call-update
  7.3 0.0 all-gather.13.cloned.1.call-start
  7.3 0.7 all-gather.13.cloned.1.call-update
  8.0 0.0 all-gather.11.cloned.1.call-start
  8.1 0.7 all-gather.11.cloned.1.call-update
  8.7 0.0 all-gather.15.cloned.1.call-start
  8.8 0.5 all-gather.15.cloned.1.call-update
  10.6 57.3 %all-gather.9.cloned.1.call-done = bf16[1,2,1024,1024]{3,2,1,0:T(8,128)(2,1)} async-done(((bf16[1,2,128,1024]{3,2,1,0:T(8,128)(2,1)}), bf16[1,2,1024,1024]{3,2,1,0:T(8,128)(2,1)}) %all-gather.9.cloned.1.call-update) | async-done | bytes 4194320 | tf_op jit(solution)/shard_map/all_gather | solution.py:26
  68.0 6.5 %bitcast_convert_fusion.1 = f32[2,1024,1024]{2,1,0:T(8,128)} fusion(bf16[1,2,1024,1024]{3,2,1,0:T(8,128)(2,1)} %all-gather.9.cloned.1.call-done), kind=kLoop, calls=%fused_computation.13 | loop fusion | flops 2097152 | bytes 12582912 | tf_op jit(solution)/shard_map/convert_element_type | solution.py:8
  74.4 8.7 %copy.9 = f32[2,1024,1024]{1,2,0:T(8,128)} copy(f32[2,1024,1024]{2,1,0:T(8,128)} %bitcast_convert_fusion.1) | data formatting | bytes 16777216 | tf_op jit(solution)/shard_map/convert_element_type | solution.py:8
  83.1 47.2 %all-gather.13.cloned.1.call-done = bf16[1,2,1024,1024]{3,2,1,0:T(8,128)(2,1)} async-done(((bf16[1,2,32,1024]{3,2,1,0:T(8,128)(2,1)}), bf16[1,2,1024,1024]{3,2,1,0:T(8,128)(2,1)}) %all-gather.13.cloned.1.call-update) | async-done | bytes 4194320 | tf_op jit(solution)/shard_map/all_gather | solution.py:35
  130.2 6.5 %bitcast_convert_fusion = f32[2,1024,1024]{2,1,0:T(8,128)} fusion(bf16[1,2,1024,1024]{3,2,1,0:T(8,128)(2,1)} %all-gather.13.cloned.1.call-done), kind=kLoop, calls=%fused_computation.11 | loop fusion | flops 2097152 | bytes 12582912 | tf_op jit(solution)/shard_map/convert_element_type | solution.py:8
  136.7 8.7 %copy.12 = f32[2,1024,1024]{1,2,0:T(8,128)} copy(f32[2,1024,1024]{2,1,0:T(8,128)} %bitcast_convert_fusion) | data formatting | bytes 16777216 | tf_op jit(solution)/shard_map/convert_element_type | solution.py:8
  145.4 0.0 copy-start
  145.4 45.9 %all-gather.11.cloned.1.call-done = bf16[2,1,1024,1024]{3,2,0,1:T(8,128)(2,1)} async-done(((bf16[2,1,32,1024]{3,2,0,1:T(8,128)(2,1)}), bf16[2,1,1024,1024]{3,2,0,1:T(8,128)(2,1)}) %all-gather.11.cloned.1.call-update) | async-done | bytes 4194320 | tf_op jit(solution)/shard_map/all_gather | solution.py:32
  191.4 12.6 %fusion.2 = f32[1024,1024,1]{1,0,2:T(8,128)} fusion(f32[2,1024,1024]{1,2,0:T(8,128)} %copy.9, bf16[2,1,1024,1024]{3,2,0,1:T(8,128)(2,1)} %all-gather.11.cloned.1.call-done, bf16[1,2,1024,1024]{3,2,1,0:T(8,128)(2,1)} %all-gather.9.cloned.1.call-done), kind=kOutput, calls=%fused_computation.4 | convolution fusion | flops 4303355904 | bytes 20971520 | tf_op jit(solution)/shard_map/kac,kcb->ab/dot_general | solution.py:29
  204.0 41.8 %all-gather.15.cloned.1.call-done = bf16[2,1,1024,1024]{3,2,0,1:T(8,128)(2,1)} async-done(((bf16[2,1,128,1024]{3,2,0,1:T(8,128)(2,1)}), bf16[2,1,1024,1024]{3,2,0,1:T(8,128)(2,1)}) %all-gather.15.cloned.1.call-update) | async-done | bytes 4194320 | tf_op jit(solution)/shard_map/all_gather | solution.py:41
  245.8 0.0 copy-done
  245.8 15.3 %fusion.8 = f32[1,1,1024,1024]{3,2,1,0:T(8,128)} fusion(f32[1024,1024,1]{1,0,2:T(8,128)} %fusion.2, f32[1,1,1024,1024]{3,2,1,0:T(8,128)} %param.8, f32[1024]{0:T(1024)S(1)} %copy-done, f32[]{:T(128)} %bitcast.14, bf16[2,1,1024,1024]{3,2,0,1:T(8,128)(2,1)} %all-gather.15.cloned.1.call-done, f32[2,1024,1024]{1,2,0:T(8,128)} %copy.12, ...), kind=kOutput, calls=%fused_computation.9 | convolution fusion | flops 4308598784 | bytes 29364228 | tf_op jit(solution)/shard_map/kac,kcb->ab/dot_general | solution.py:38
Async XLA Ops:
  6.5 61.4 %all-gather.9.cloned.1.call-start = ((), (), s32[]{:S(2)}) async-start(), calls=%async_computation | async-start | bytes 4718592 | tf_op jit(solution)/shard_map/all_gather | solution.py:26
  7.3 123.0 %all-gather.13.cloned.1.call-start = ((), (), s32[]{:S(2)}) async-start(), calls=%async_computation.2 | async-start | bytes 4325376 | tf_op jit(solution)/shard_map/all_gather | solution.py:35
  8.0 183.4 %all-gather.11.cloned.1.call-start = ((), (), s32[]{:S(2)}) async-start(), calls=%async_computation.1 | async-start | bytes 4325376 | tf_op jit(solution)/shard_map/all_gather | solution.py:32
  8.7 237.0 %all-gather.15.cloned.1.call-start = ((), (), s32[]{:S(2)}) async-start(), calls=%async_computation.3 | async-start | bytes 4718592 | tf_op jit(solution)/shard_map/all_gather | solution.py:41
  145.4 100.3 %copy-start = (f32[1024]{0:T(1024)S(1)}, f32[1024]{0:T(1024)}, u32[]{:S(2)}) copy-start(f32[1024]{0:T(1024)} %param.15) | copy-start | bytes 12292
Sparse Core Ops, SparseCore 0:
  9.1 58.7 all-gather.8
  70.6 59.5 all-gather.12
  132.9 58.4 all-gather.10
  193.0 52.7 all-gather.14
where the time goes:
time: 268 us
  waiting for transfers between devices  195 us (73%)
  matrix products  27.9 us (10%)
  local copies, waits for them, and re-layouts  17.4 us (6%)
  between operations  14.4 us (5%)
  other arithmetic  12.9 us (5%)
    all_gather x1, waiting for transfers between devices, body(): left_whole = lax.all_gather(left_slab, 'col', axis=1, tiled=True)  57.3 us
    all_gather x1, waiting for transfers between devices, body(): right_whole = lax.all_gather(right_slab, 'row', axis=1, tiled=True)  47.2 us
    all_gather x1, waiting for transfers between devices, body(): lax.all_gather(right_weight_slab, 'row', axis=1, tiled=True)  45.9 us
    all_gather x1, waiting for transfers between devices, body(): lax.all_gather(left_weight_slab, 'col', axis=1, tiled=True)  41.8 us
    convert_element_type x2, local copies, waits for them, and re-layouts, combine_blocks(): as_float = blocks.astype(jnp.float32)  17.4 us
    dot_general x1, matrix products, body(): jnp.einsum('kac,kcb->ab', mixed_cols, lax.all_gather(left_weight_slab, 'c...  15.3 us
    convert_element_type x2, other arithmetic, combine_blocks(): as_float = blocks.astype(jnp.float32)  12.9 us
    dot_general x1, matrix products, body(): jnp.einsum('kac,kcb->ab', mixed_cols, lax.all_gather(right_weight_slab, '...  12.6 us
  transfers between devices with their start and end apart: 4, of which 4 were waited for; matrix products, arithmetic and copies ran while one was open for 16% of the time, Pallas kernels for 0%

commit v1 on v0

--- a/solution.py
+++ b/solution.py
@@ -23,7 +23,8 @@
     right_slab = panels_right[0]
     right_weight_slab = weights_right[:, 0]
     left_weight_slab = weights_left[:, 0]
-    left_whole = lax.all_gather(left_slab, "col", axis=1, tiled=True)
+    answer_strips_all = lambda vals: jnp.concatenate(lax.all_gather(vals, axis_name="col"), axis=1)
+    left_whole = answer_strips_all(left_slab)
     left_mixed = combine_blocks(left_whole)
     mixed_cols = left_mixed
     direct = jnp.einsum(

time: 268 us -> 267 us (level)
  other arithmetic: 12.9 us -> 23 us
  waiting for transfers between devices: 195 us -> 186 us
    all_gather x1, waiting for transfers between devices: 47.2 us -> 37.1 us  [body(): right_whole = lax.all_gather(right_slab, 'row', axis=1, tiled=True)]
    convert_element_type x0 -> x1, other arithmetic: none -> 10 us  [combine_blocks(): (2.0 * as_float - jnp.swapaxes(as_float, -1, -2)).astype(jnp.bfloat16)]
    all_gather x1, waiting for transfers between devices: 45.9 us -> 49.7 us  [body(): lax.all_gather(right_weight_slab, 'row', axis=1, tiled=True)]
    dot_general x1, matrix products: 15.3 us -> 12.4 us  [body(): jnp.einsum('kac,kcb->ab', mixed_cols, lax.all_gather(left_weight_slab, 'c...]
  transfers between devices with their start and end apart: 4 -> 4, of which waited for: 4 -> 4; matrix products, arithmetic and copies ran while one was open for 16% -> 20% of each run, Pallas kernels for 0% -> 0%
where the time goes in v1:
time: 267 us; the launch traced here: 266 us
  waiting for transfers between devices  186 us (70%)
  matrix products  25.3 us (9%)
  other arithmetic  23 us (9%)
  local copies, waits for them, and re-layouts  17.4 us (7%)
  between operations  14.4 us (5%)
    all_gather x1, waiting for transfers between devices, body(): lax.all_gather(vals, axis_name='col')  57.3 us
    all_gather x1, waiting for transfers between devices, body(): lax.all_gather(right_weight_slab, 'row', axis=1, tiled=True)  49.7 us
    all_gather x1, waiting for transfers between devices, body(): lax.all_gather(left_weight_slab, 'col', axis=1, tiled=True)  39.3 us
    all_gather x1, waiting for transfers between devices, body(): right_whole = lax.all_gather(right_slab, 'row', axis=1, tiled=True)  37.1 us
    convert_element_type x2, local copies, waits for them, and re-layouts, combine_blocks(): as_float = blocks.astype(jnp.float32)  17.4 us
    convert_element_type x2, other arithmetic, combine_blocks(): as_float = blocks.astype(jnp.float32)  12.9 us
    dot_general x1, matrix products, body(): jnp.einsum('kac,kcb->ab', mixed_cols, lax.all_gather(right_weight_slab, '...  12.9 us
    dot_general x1, matrix products, body(): jnp.einsum('kac,kcb->ab', mixed_cols, lax.all_gather(left_weight_slab, 'c...  12.4 us
  transfers between devices with their start and end apart: 4, of which 4 were waited for; matrix products, arithmetic and copies ran while one was open for 20% of the time, Pallas kernels for 0%

profile of v1, /device:TPU:1, one launch (start us, length us, event | category | flops | bytes accessed | tf_op | source)
XLA Modules:
  0.0 266.4 jit_solution(4692943343791728522)
XLA Ops:
  6.5 0.0 all-gather.8.cloned.1.call-start
  6.5 0.7 all-gather.8.cloned.1.call-update
  7.3 0.0 all-gather.12.cloned.1.call-start
  7.3 0.7 all-gather.12.cloned.1.call-update
  8.0 0.0 all-gather.14.cloned.1.call-start
  8.1 0.7 all-gather.14.cloned.1.call-update
  8.7 0.0 all-gather.10.cloned.1.call-start
  8.8 0.5 all-gather.10.cloned.1.call-update
  10.6 57.3 %all-gather.8.cloned.1.call-done = bf16[8,2,128,1024]{3,2,1,0:T(8,128)(2,1)} async-done(((bf16[1,2,128,1024]{3,2,1,0:T(8,128)(2,1)}), bf16[8,2,128,1024]{3,2,1,0:T(8,128)(2,1)}) %all-gather.8.cloned.1.call-update) | async-done | bytes 4194320 | tf_op jit(solution)/shard_map/all_gather | solution.py:26
  67.9 6.5 %copy_convert_fusion = f32[8,2,128,1024]{3,2,0,1:T(8,128)} fusion(bf16[8,2,128,1024]{3,2,1,0:T(8,128)(2,1)} %all-gather.8.cloned.1.call-done), kind=kLoop, calls=%fused_computation.13 | loop fusion | flops 2097152 | bytes 12582912 | tf_op jit(solution)/shard_map/convert_element_type | solution.py:8
  74.4 8.7 %copy.25 = f32[2,1024,1024]{1,2,0:T(8,128)} copy(f32[2,1024,1024]{2,1,0:T(8,128)} %bitcast.47) | data formatting | bytes 16777216 | tf_op jit(solution)/shard_map/convert_element_type | solution.py:8
  83.1 10.0 %fusion = bf16[2,1024,1024]{1,2,0:T(8,128)(2,1)} fusion(f32[8,2,128,1024]{3,2,0,1:T(8,128)} %copy_convert_fusion, f32[2,1024,1024]{1,2,0:T(8,128)} %copy.25), kind=kLoop, calls=%fused_computation.1 | loop fusion | flops 6291456 | bytes 20971520 | tf_op jit(solution)/shard_map/convert_element_type | solution.py:9
  93.1 37.1 %all-gather.12.cloned.1.call-done = bf16[1,2,1024,1024]{3,2,1,0:T(8,128)(2,1)} async-done(((bf16[1,2,32,1024]{3,2,1,0:T(8,128)(2,1)}), bf16[1,2,1024,1024]{3,2,1,0:T(8,128)(2,1)}) %all-gather.12.cloned.1.call-update) | async-done | bytes 4194320 | tf_op jit(solution)/shard_map/all_gather | solution.py:36
  130.2 6.5 %bitcast_convert_fusion = f32[2,1024,1024]{2,1,0:T(8,128)} fusion(bf16[1,2,1024,1024]{3,2,1,0:T(8,128)(2,1)} %all-gather.12.cloned.1.call-done), kind=kLoop, calls=%fused_computation.10 | loop fusion | flops 2097152 | bytes 12582912 | tf_op jit(solution)/shard_map/convert_element_type | solution.py:8
  136.7 8.7 %copy.28 = f32[2,1024,1024]{1,2,0:T(8,128)} copy(f32[2,1024,1024]{2,1,0:T(8,128)} %bitcast_convert_fusion) | data formatting | bytes 16777216 | tf_op jit(solution)/shard_map/convert_element_type | solution.py:8
  145.5 0.0 copy-start
  145.5 39.3 %all-gather.14.cloned.1.call-done = bf16[2,1,1024,1024]{3,2,0,1:T(8,128)(2,1)} async-done(((bf16[2,1,128,1024]{3,2,0,1:T(8,128)(2,1)}), bf16[2,1,1024,1024]{3,2,0,1:T(8,128)(2,1)}) %all-gather.14.cloned.1.call-update) | async-done | bytes 4194320 | tf_op jit(solution)/shard_map/all_gather | solution.py:42
  184.8 12.4 %fusion.2 = f32[1024,1024,1]{0,1,2:T(8,128)} fusion(f32[2,1024,1024]{1,2,0:T(8,128)} %copy.28, bf16[2,1,1024,1024]{3,2,0,1:T(8,128)(2,1)} %all-gather.14.cloned.1.call-done, bf16[1,2,1024,1024]{3,2,1,0:T(8,128)(2,1)} %all-gather.12.cloned.1.call-done), kind=kOutput, calls=%fused_computation.4 | convolution fusion | flops 4303355904 | bytes 20971520 | tf_op jit(solution)/shard_map/kac,kcb->ab/dot_general | solution.py:39
  197.2 49.7 %all-gather.10.cloned.1.call-done = bf16[2,1,1024,1024]{3,2,0,1:T(8,128)(2,1)} async-done(((bf16[2,1,32,1024]{3,2,0,1:T(8,128)(2,1)}), bf16[2,1,1024,1024]{3,2,0,1:T(8,128)(2,1)}) %all-gather.10.cloned.1.call-update) | async-done | bytes 4194320 | tf_op jit(solution)/shard_map/all_gather | solution.py:33
  246.9 0.0 copy-done
  246.9 12.9 %fusion.6 = f32[1,1,1024,1024]{3,2,1,0:T(8,128)} fusion(f32[1024,1024,1]{0,1,2:T(8,128)} %fusion.2, f32[1,1,1024,1024]{3,2,1,0:T(8,128)} %param.8, f32[1024]{0:T(1024)S(1)} %copy-done, f32[]{:T(128)} %bitcast.15, bf16[2,1024,1024]{1,2,0:T(8,128)(2,1)} %fusion, bf16[2,1,1024,1024]{3,2,0,1:T(8,128)(2,1)} %all-gather.10.cloned.1.call-done), kind=kOutput, calls=%fused_computation.8 | convolution fusion | flops 4300210176 | bytes 20975620 | tf_op jit(solution)/shard_map/kac,kcb->ab/dot_general | solution.py:30
Async XLA Ops:
  6.5 61.4 %all-gather.8.cloned.1.call-start = ((), (), s32[]{:S(2)}) async-start(), calls=%async_computation | async-start | bytes 4718592 | tf_op jit(solution)/shard_map/all_gather | solution.py:26
  7.3 123.0 %all-gather.12.cloned.1.call-start = ((), (), s32[]{:S(2)}) async-start(), calls=%async_computation.2 | async-start | bytes 4325376 | tf_op jit(solution)/shard_map/all_gather | solution.py:36
  8.0 176.8 %all-gather.14.cloned.1.call-start = ((), (), s32[]{:S(2)}) async-start(), calls=%async_computation.3 | async-start | bytes 4718592 | tf_op jit(solution)/shard_map/all_gather | solution.py:42
  8.7 238.2 %all-gather.10.cloned.1.call-start = ((), (), s32[]{:S(2)}) async-start(), calls=%async_computation.1 | async-start | bytes 4325376 | tf_op jit(solution)/shard_map/all_gather | solution.py:33
  145.5 101.5 %copy-start = (f32[1024]{0:T(1024)S(1)}, f32[1024]{0:T(1024)}, u32[]{:S(2)}) copy-start(f32[1024]{0:T(1024)} %param.15) | copy-start | bytes 12292
Sparse Core Ops, SparseCore 0:
  9.1 58.7 all-gather.7
  70.6 59.5 all-gather.11
  132.0 52.7 all-gather.13
  187.3 59.5 all-gather.9
